TPU v7x, 32 devices: a whole 2x2x4 slice. The times are simulated.
32 devices in a mesh: gx: 4 (over x, core), gy: 4 (over z), gz: 2 (over y).
Axes of the slice: x: 2, y: 2, z: 4, core: 2. Of those that a mesh axis runs over, the one named last changes fastest.
Arguments:
- layer_input: bfloat16 [1024, 4096], P('gz', ('gx', 'gy')), may hold values from -6 to 6
- modality: int32 [1024], P('gz'), may hold values 0 or 1
- image_spans: int32 [2, 8], replicated, may hold values from 0 to 1024, as said below
- norm_gain: float32 [2, 4096], P(None, ('gx', 'gy')), may hold values from 0.1 to 1.9
- w_qkv: bfloat16 [3, 4096, 2048], P(None, 'gz', ('gx', 'gy')), as said below
- w_out: bfloat16 [2048, 4096], P(('gx', 'gy'), 'gz'), may hold values from -0.125 to 0.125
- grad_out: bfloat16 [1024, 4096], P('gz', ('gx', 'gy')), may hold values from -6 to 6
Outputs:
- attn_out: bfloat16 [1024, 4096], P('gz', ('gx', 'gy'))
- grad_in: bfloat16 [1024, 4096], P('gz', ('gx', 'gy'))
- grad_qkv: float32 [3, 4096, 2048], P(None, 'gz', ('gx', 'gy'))
- grad_wout: float32 [2048, 4096], P(('gx', 'gy'), 'gz')
- grad_gain: float32 [2, 4096], P(None, ('gx', 'gy'))
Inputs may be any that keep to these rules, and one draw needn't show every extreme that they name: `image_spans`: row 0 holds the first position of each of 8 image spans, in increasing order, and row 1 one past its last; spans are disjoint and none is empty. `w_qkv`: entries are at most 20 * 4096 ** -0.5 in magnitude.
All inputs are finite; a program needn't handle non-finite values. No bound on the sum of `modality` on one device may be relied on, other than what follows from the above.
Results may differ from a plain program's by a relative error of at most 0.035.
The roundings to bfloat16 on the way count: a program that leaves them out, or rounds other values in their place, can miss the bound.
Values may be sent and summed in bfloat16 or wider, within the bound.
A program may use at most 128 MiB of HBM per device.

v0:
```python
import math
import jax
import jax.numpy as jnp
from jax import lax
from jax.sharding import PartitionSpec as P

epsilon = 1e-05
masked_low = -1e30


def span_index(positions, image_spans):
    inside = (positions[:, None] >= image_spans[0][None, :]) & (
        positions[:, None] < image_spans[1][None, :]
    )
    labels = jnp.arange(1, image_spans.shape[1] + 1, dtype=jnp.int32)
    return jnp.sum(jnp.where(inside, labels[None, :], 0), axis=1) - 1


def visible(query_pos, query_span, key_pos, key_span):
    causal = key_pos[None, :] <= query_pos[:, None]
    same_image = (query_span[:, None] == key_span[None, :]) & (query_span[:, None] >= 0)
    return causal | same_image


def per_device(layer_input, modality, image_spans, norm_gain, w_qkv, w_out, grad_out):
    tok_rows, local_width = layer_input.shape
    full_width = local_width * lax.axis_size(("gx", "gy"))
    head_dim = w_qkv.shape[2]
    inputs_f = layer_input.astype(jnp.float32)
    squares = lax.psum(jnp.sum(inputs_f * inputs_f, axis=1), ("gx", "gy"))
    inv_rms = lax.rsqrt(squares / full_width + epsilon)
    row_gain = jnp.where(modality[:, None] == 1, norm_gain[1][None, :], norm_gain[0][None, :])
    scaled = inputs_f * inv_rms[:, None]
    normed = (scaled * row_gain).astype(jnp.bfloat16)
    w_full = lax.all_gather(w_qkv, "gz", axis=1, tiled=True)
    wo_full = lax.all_gather(w_out, "gz", axis=1, tiled=True)
    rows_block = w_full
    projected = jnp.einsum(
        "tc,mch->mth",
        lax.all_gather(normed, ("gx", "gy"), axis=1, tiled=True),
        rows_block,
        preferred_element_type=jnp.float32,
    )
    projected = projected.astype(jnp.bfloat16)
    queries = projected[0]
    keys_values = lax.all_gather(
        jnp.concatenate([projected[1], projected[2]], axis=1), "gz", axis=0, tiled=True
    )
    key_total = keys_values.shape[0]
    query_pos = lax.axis_index("gz") * tok_rows + jnp.arange(tok_rows, dtype=jnp.int32)
    query_span = span_index(query_pos, image_spans)
    key_block = 512
    block_count = key_total // key_block
    score_scale = 1.0 / math.sqrt(head_dim)
    block_ids = jnp.arange(block_count, dtype=jnp.int32)

    def block_scores(block_idx):
        first_key = block_idx * key_block
        kv_block = lax.dynamic_slice_in_dim(keys_values, first_key, key_block, 0)
        key_pos = first_key + jnp.arange(key_block, dtype=jnp.int32)
        allowed = visible(query_pos, query_span, key_pos, span_index(key_pos, image_spans))
        scores = (
            lax.dot_general(
                queries,
                kv_block[:, :head_dim],
                (((1,), (1,)), ((), ())),
                preferred_element_type=jnp.float32,
            )
            * score_scale
        )
        return (kv_block, allowed, scores)

    def gather_stats(state, block_idx):
        maxima, summed = state
        kv_block, allowed, scores = block_scores(block_idx)
        new_maxima = jnp.maximum(maxima, jnp.max(jnp.where(allowed, scores, masked_low), axis=1))
        fresh = jnp.sum(jnp.where(allowed, jnp.exp(scores - new_maxima[:, None]), 0.0), axis=1)
        return ((new_maxima, summed * jnp.exp(maxima - new_maxima) + fresh), None)

    start_state = (
        jnp.full((tok_rows,), masked_low, jnp.float32),
        jnp.zeros((tok_rows,), jnp.float32),
    )
    (maxima, summed), unused = lax.scan(gather_stats, start_state, block_ids)
    lse = maxima + jnp.log(summed)

    def block_probs(block_idx):
        kv_block, allowed, scores = block_scores(block_idx)
        return (kv_block, jnp.where(allowed, jnp.exp(scores - lse[:, None]), 0.0))

    def attend(accum, block_idx):
        kv_block, attn_p = block_probs(block_idx)
        return (
            accum
            + jnp.dot(
                attn_p.astype(jnp.bfloat16),
                kv_block[:, head_dim:],
                preferred_element_type=jnp.float32,
            ),
            None,
        )

    attended_f, unused = lax.scan(attend, jnp.zeros((tok_rows, head_dim), jnp.float32), block_ids)
    attended = attended_f.astype(jnp.bfloat16)
    all_heads = lax.all_gather(attended, ("gx", "gy"), axis=1, tiled=True)
    out_rows = lax.all_to_all(wo_full, ("gx", "gy"), split_axis=1, concat_axis=0, tiled=True)
    head_total = out_rows.shape[0] // head_dim
    per_head = jnp.einsum(
        "thd,hdc->htc",
        all_heads.reshape(tok_rows, head_total, head_dim),
        out_rows.reshape(head_total, head_dim, local_width),
        preferred_element_type=jnp.float32,
    )
    per_head = lax.optimization_barrier(per_head.astype(jnp.bfloat16)).astype(jnp.float32)
    attn_out = jnp.sum(per_head, axis=0).astype(jnp.bfloat16)
    segment = lax.all_gather(grad_out, ("gx", "gy"), axis=1, tiled=True)
    d_accum = lax.dot_general(
        segment, wo_full, (((1,), (1,)), ((), ())), preferred_element_type=jnp.float32
    )
    partial_value = lax.dot_general(
        attended, segment, (((0,), (0,)), ((), ())), preferred_element_type=jnp.float32
    )
    d_attended = d_accum.astype(jnp.bfloat16)
    row_dots = jnp.sum(d_attended.astype(jnp.float32) * attended.astype(jnp.float32), axis=1)

    def backward_block(d_query, block_idx):
        kv_block, attn_p = block_probs(block_idx)
        d_probs = lax.dot_general(
            d_attended,
            kv_block[:, head_dim:],
            (((1,), (1,)), ((), ())),
            preferred_element_type=jnp.float32,
        )
        d_scores = (attn_p * (d_probs - row_dots[:, None]) * score_scale).astype(jnp.bfloat16)
        d_query = d_query + jnp.dot(
            d_scores, kv_block[:, :head_dim], preferred_element_type=jnp.float32
        )
        d_keys = lax.dot_general(
            d_scores, queries, (((0,), (0,)), ((), ())), preferred_element_type=jnp.float32
        )
        d_values = lax.dot_general(
            attn_p.astype(jnp.bfloat16),
            d_attended,
            (((0,), (0,)), ((), ())),
            preferred_element_type=jnp.float32,
        )
        return (d_query, jnp.concatenate([d_keys, d_values], axis=1))

    d_query_f, kv_parts = lax.scan(
        backward_block, jnp.zeros((tok_rows, head_dim), jnp.float32), block_ids
    )
    kv_grad = lax.psum_scatter(
        kv_parts.reshape(key_total, 2 * head_dim).astype(jnp.bfloat16),
        "gz",
        scatter_dimension=0,
        tiled=True,
    ).astype(jnp.float32)
    grads = jnp.stack(
        [
            d_query_f.astype(jnp.bfloat16),
            kv_grad[:, :head_dim].astype(jnp.bfloat16),
            kv_grad[:, head_dim:].astype(jnp.bfloat16),
        ]
    )
    w_grad = jnp.einsum(
        "tc,mth->mch",
        lax.all_gather(normed, ("gx", "gy"), axis=1, tiled=True),
        grads,
        preferred_element_type=jnp.float32,
    )
    grad_qkv, grad_wout = (
        lax.psum_scatter(w_grad.astype(jnp.bfloat16), "gz", scatter_dimension=1, tiled=True).astype(
            jnp.float32
        ),
        lax.psum_scatter(
            partial_value.astype(jnp.bfloat16), "gz", scatter_dimension=1, tiled=True
        ).astype(jnp.float32),
    )
    rows_block = w_full
    grad_normed = (
        lax.psum_scatter(
            jnp.einsum("mch,mth->ct", rows_block, grads, preferred_element_type=jnp.float32).astype(
                jnp.bfloat16
            ),
            ("gx", "gy"),
            scatter_dimension=0,
            tiled=True,
        )
        .astype(jnp.float32)
        .T
    )
    upstream = grad_normed * row_gain
    norm_dots = lax.psum(jnp.sum(upstream * scaled, axis=1), ("gx", "gy"))
    grad_in = (inv_rms[:, None] * (upstream - scaled * (norm_dots / full_width)[:, None])).astype(
        jnp.bfloat16
    )
    onehot = (modality[:, None] == jnp.arange(2, dtype=jnp.int32)[None, :]).astype(jnp.float32)
    local_gain = jnp.dot(onehot.T, grad_normed * scaled, precision=lax.Precision.HIGHEST)
    grad_gain = lax.psum(local_gain, "gz")
    return (attn_out, grad_in, grad_qkv, grad_wout, grad_gain)


def solution(mesh):
    in_specs = (
        P("gz", ("gx", "gy")),
        P("gz"),
        P(),
        P(None, ("gx", "gy")),
        P(None, "gz", ("gx", "gy")),
        P(("gx", "gy"), "gz"),
        P("gz", ("gx", "gy")),
    )
    out_specs = (
        P("gz", ("gx", "gy")),
        P("gz", ("gx", "gy")),
        P(None, "gz", ("gx", "gy")),
        P(("gx", "gy"), "gz"),
        P(None, ("gx", "gy")),
    )
    return jax.shard_map(
        per_device, mesh=mesh, in_specs=in_specs, out_specs=out_specs, check_vma=False
    )
```

profile of v0, /device:TPU:0, one launch (start us, length us, event | category | flops | bytes accessed | tf_op | source)
XLA Modules:
  0.0 420.7 jit_solution(4267195177550142330)
XLA Ops:
  7.3 2.7 copy.44
  10.0 0.1 fusion.65
  10.2 35.2 %psum.21 = f32[512]{0:T(512)S(1)} all-reduce(f32[512]{0:T(512)S(1)} %fusion.65), channel_id=1, replica_groups=mesh['gx'=4,'gy'=4,'gz'=2] {'gx','gy'}, use_global_device_ids=true, to_apply=%region_1.0 | all-reduce | flops 512 | bytes 4096 | tf_op jit(solution)/shard_map/psum | solution.py:30
  45.4 0.9 fusion.66
  46.4 1.0 copy.50
  47.5 0.5 all-gather.14.cloned.1.call-update
  48.3 9.5 %all-gather.8.cloned.1.call-done = bf16[3,4096,128]{1,2,0:T(8,128)(2,1)} async-done(((bf16[3,2048,128]{1,2,0:T(8,128)(2,1)}), bf16[3,4096,128]{1,2,0:T(8,128)(2,1)}) %all-gather.8.cloned.1.call-update) | async-done | bytes 3145744 | tf_op jit(solution)/shard_map/all_gather | solution.py:35
  57.8 55.2 %all-gather.6.cloned.1.call-done = bf16[512,4096]{1,0:T(8,128)(2,1)} async-done(((bf16[512,256]{1,0:T(8,128)(2,1)}), bf16[512,4096]{1,0:T(8,128)(2,1)}) %all-gather.6.cloned.1.call-update) | async-done | bytes 4194320 | tf_op jit(solution)/shard_map/all_gather | solution.py:40
  113.0 5.0 %fusion.75 = f32[512,384]{0,1:S(1)} fusion(bf16[512,4096]{1,0:T(8,128)(2,1)} %all-gather.6.cloned.1.call-done, bf16[4096,384]{0,1:T(8,128)(2,1)} %bitcast.156), kind=kOutput, calls=%fused_computation.134 | convolution fusion | flops 1610612736 | bytes 8126464
  118.1 13.9 %all_gather.21 = bf16[1024,256]{0,1:T(8,128)(2,1)S(1)} all-gather(bf16[512,256]{0,1:T(8,128)(2,1)S(1)} %pad_maximum_fusion.1), channel_id=1, replica_groups=mesh['gx'=4,'gy'=4,'gz'=2] {'gz'}, dimensions={0}, use_global_device_ids=true | all-gather | bytes 786432 | tf_op jit(solution)/shard_map/all_gather | solution.py:46
  132.0 0.2 copy.47
  132.4 4.8 %while.43 = (s32[]{:T(128)}, f32[512]{0:T(512)S(1)}, f32[512]{0:T(512)S(1)}, s32[2]{0:T(128)S(1)}, s32[512]{0:T(512)S(1)}, /*index=5*/s32[2,8]{1,0:T(2,128)S(1)}...) while((s32[]{:T(128)}, f32[512]{0:T(512)S(1)}, ...), condition=%wide.region_7.8_spmd.clone, body=%wide.region_3.7_spmd.clone.sunk | while | flops 70803472 | bytes 2418638 | solution.py:84
  132.4 0.6 dynamic_slice.46
  133.7 0.5 select_reduce_fusion.12
  134.2 0.5 select_reduce_fusion.13
  134.8 0.6 dynamic_slice.46
  136.1 0.5 select_reduce_fusion.12
  136.6 0.5 select_reduce_fusion.13
  137.2 0.6 log_add_fusion
  137.7 5.9 %while.44 = (s32[]{:T(128)}, f32[512,128]{1,0:T(8,128)S(1)}, s32[2]{0:T(128)S(1)}, s32[512]{0:T(512)S(1)}, s32[2,8]{1,0:T(2,128)S(1)}, /*index=5*/bf16[1024,256]...) while((s32[]{:T(128)}, f32[512,128]{1,0:T(8,128)S(1)}, ...), condition=%wide.region_10.11_spmd.clone, body=%wide.region_8.10_spmd.clone.sunk | while | flops 136467984 | bytes 945628 | solution.py:103
  137.7 0.6 dynamic_slice.47
  139.1 1.5 fusion.118
  140.7 0.6 dynamic_slice.47
  142.1 1.5 fusion.118
  143.8 47.6 %all-gather.14.cloned.1.call-done = bf16[512,4096]{1,0:T(8,128)(2,1)} async-done(((bf16[512,256]{1,0:T(8,128)(2,1)}), bf16[512,4096]{1,0:T(8,128)(2,1)}) %all-gather.14.cloned.1.call-update) | async-done | bytes 4194320 | tf_op jit(solution)/shard_map/all_gather | solution.py:116
  191.3 4.0 multiply_reduce_fusion
  195.5 0.5 iota.88
  196.0 9.3 %while.45 = (s32[]{:T(128)}, f32[512,128]{1,0:T(8,128)S(1)}, bf16[2,512,256]{1,2,0:T(8,128)(2,1)S(1)}, s32[2]{0:T(128)}, s32[512]{0:T(512)S(1)}, /*index=5*/s32[...) while((s32[]{:T(128)}, f32[512,128]{1,0:T(8,128)S(1)}, ...), condition=%wide.region_15.16_spmd.clone, body=%wide.region_13.15_spmd.clone.sunk | while | flops 339367424 | bytes 6974985 | solution.py:149
  196.0 1.2 dynamic_slice.48
  198.0 1.2 fusion.129
  199.3 0.3 fusion.130
  199.6 0.3 fusion.132
  199.9 0.3 fusion.131
  200.2 0.4 convolution_add_fusion.2
  200.6 1.2 dynamic_slice.48
  202.7 1.2 fusion.129
  203.9 0.3 fusion.130
  204.2 0.3 fusion.132
  204.5 0.3 fusion.131
  204.9 0.4 convolution_add_fusion.2
  205.3 1.0 copy.56
  206.4 3.9 convolution_convert_fusion.1
  210.3 0.7 all-gather.10.cloned.1.call-update
  211.1 8.2 %reduce-scatter.5.cloned.1.call-done = bf16[512,256]{1,0:T(8,128)(2,1)} async-done(((bf16[1024,256]{1,0:T(8,128)(2,1)}), bf16[512,256]{1,0:T(8,128)(2,1)}) %reduce-scatter.5.cloned.1.call-update) | async-done | bytes 262160 | tf_op jit(solution)/shard_map/reduce_scatter | solution.py:152
  219.2 1.0 slice_bitcast_fusion.7
  220.2 5.8 %fusion.52 = bf16[4096,512]{0,1:T(8,128)(2,1)} fusion(bf16[3,4096,128]{1,2,0:T(8,128)(2,1)} %all-gather.8.cloned.1.call-done, bf16[1,512,128]{2,1,0:T(8,128)(2,1)S(1)} %get-tuple-element.678, bf16[1,512,128]{2,1,0:T(8,128)(2,1)S(1)} %get-tuple-element.677, bf16[1,512,128]{2,1,0:T(8,128)(2,1)S(1)} %convert_bitcast_fusion.1), kind=kOutput, calls=%fused_computation.84 | convolution fusion | flops 1613103104 | bytes 7733248 | tf_op jit(solution)/shard_map/mch,mth->ct/dot_general | solution.py:182
  226.1 0.2 reduce-scatter.9.cloned.1.call-start
  226.3 6.1 %fusion.53 = bf16[3,4096,128]{1,2,0:T(8,128)(2,1)} fusion(bf16[512,4096]{1,0:T(8,128)(2,1)} %all-gather.6.cloned.1.call-done, bf16[1,512,128]{2,1,0:T(8,128)(2,1)S(1)} %get-tuple-element.678, bf16[1,512,128]{2,1,0:T(8,128)(2,1)S(1)} %get-tuple-element.677, bf16[1,512,128]{2,1,0:T(8,128)(2,1)S(1)} %convert_bitcast_fusion.1), kind=kOutput, calls=%fused_computation.85 | convolution fusion | flops 1612578816 | bytes 7733248 | tf_op jit(solution)/shard_map/tc,mth->mch/dot_general | solution.py:165
  232.4 1.3 copy.51
  233.8 5.5 %all-to-all-start = ((bf16[128,16,256]{2,0,1:T(8,128)(2,1)}), bf16[128,16,256]{2,0,1:T(8,128)(2,1)S(1)}, u32[]{:S(2)}, u32[]{:S(2)}) async-start(bf16[128,16,256]{2,0,1:T(8,128)(2,1)} %copy.51), calls=%async_computation | async-start | bytes 2097152 | tf_op jit(solution)/shard_map/all_to_all | solution.py:106
  239.3 3.1 reduce-scatter.11.cloned.1.call-done
  242.4 2.1 convert_element_type.104
  244.5 25.8 %all-to-all-done = bf16[128,16,256]{2,0,1:T(8,128)(2,1)S(1)} async-done(((bf16[128,16,256]{2,0,1:T(8,128)(2,1)}), bf16[128,16,256]{2,0,1:T(8,128)(2,1)S(1)}, u32[]{:S(2)}, u32[]{:S(2)}) %all-to-all-start) | async-done | bytes 1048608 | tf_op jit(solution)/shard_map/all_to_all | solution.py:106
  270.3 19.1 %all-gather.10.cloned.1.call-done = bf16[512,2048]{0,1:T(8,128)(2,1)} async-done(((bf16[512,128]{0,1:T(8,128)(2,1)}), bf16[512,2048]{0,1:T(8,128)(2,1)}) %all-gather.10.cloned.1.call-update) | async-done | bytes 2097168 | tf_op jit(solution)/shard_map/all_gather | solution.py:105
  289.4 4.8 %convolution_convert_fusion.2 = bf16[16,512,256]{2,1,0:T(8,128)(2,1)} fusion(bf16[512,16,128]{0,2,1:T(8,128)(2,1)} %bitcast.147, bf16[128,16,256]{2,0,1:T(8,128)(2,1)S(1)} %all-to-all-done), kind=kOutput, calls=%fused_computation.88 | convolution fusion | flops 538968064 | bytes 7340032 | tf_op jit(solution)/shard_map/thd,hdc->htc/dot_general | solution.py:108
  294.2 3.5 reduce_sum.98
  297.8 67.0 %reduce-scatter.7.cloned.1.call-done = bf16[256,512]{0,1:T(8,128)(2,1)} async-done(((bf16[4096,512]{0,1:T(8,128)(2,1)}), bf16[256,512]{0,1:T(8,128)(2,1)}) %reduce-scatter.7.cloned.1.call-update) | async-done | bytes 262160 | tf_op jit(solution)/shard_map/reduce_scatter | solution.py:181
  364.8 1.3 fusion.59
  366.1 30.5 %psum.22 = f32[512]{0:T(512)S(1)} all-reduce(f32[512]{0:T(512)S(1)} %fusion.59), channel_id=1, replica_groups=mesh['gx'=4,'gy'=4,'gz'=2] {'gx','gy'}, use_global_device_ids=true, to_apply=%region_19.20 | all-reduce | flops 512 | bytes 4096 | tf_op jit(solution)/shard_map/psum | solution.py:193
  396.6 1.5 fusion.63
  398.1 5.7 %psum.23 = f32[2,256]{1,0:T(2,128)} all-reduce(f32[2,256]{1,0:T(2,128)S(1)} %fusion.63), channel_id=1, replica_groups=mesh['gx'=4,'gy'=4,'gz'=2] {'gz'}, use_global_device_ids=true, to_apply=%region_22.23 | all-reduce | flops 512 | bytes 4096 | tf_op jit(solution)/shard_map/psum | solution.py:199
  403.8 6.4 %reduce-scatter.9.cloned.1.call-done = bf16[3,2048,128]{1,2,0:T(8,128)(2,1)} async-done(((bf16[3,4096,128]{1,2,0:T(8,128)(2,1)}), bf16[3,2048,128]{1,2,0:T(8,128)(2,1)}) %reduce-scatter.9.cloned.1.call-update) | async-done | bytes 1572880 | tf_op jit(solution)/shard_map/reduce_scatter | solution.py:172
  410.2 3.1 copy.59
  413.2 1.0 fusion.62
  (113 shorter events, 1.9 us)
Async XLA Ops:
  7.2 2.8 copy-start
  7.2 38.2 %copy-start.12 = (s32[512]{0:T(512)S(1)}, s32[512]{0:T(512)}, u32[]{:S(2)}) copy-start(s32[512]{0:T(512)} %param.14) | copy-start | bytes 6148
  7.2 38.2 %copy-start.14 = (f32[2,256]{1,0:T(2,128)S(1)}, f32[2,256]{1,0:T(2,128)}, u32[]{:S(2)}) copy-start(f32[2,256]{1,0:T(2,128)} %param.16) | copy-start | bytes 6148
  7.2 39.2 %copy-start.4 = (bf16[128,2048]{1,0:T(8,128)(2,1)S(1)}, bf16[128,2048]{1,0:T(8,128)(2,1)}, u32[]{:S(2)}) copy-start(bf16[128,2048]{1,0:T(8,128)(2,1)} %param.18) | copy-start | bytes 1572868
  7.2 41.0 %copy-start.5 = (s32[2,8]{1,0:T(2,128)S(1)}, s32[2,8]{1,0:T(2,128)}, u32[]{:S(2)}) copy-start(s32[2,8]{1,0:T(2,128)} %param.15) | copy-start | bytes 196
  7.2 50.6 %all-gather.8.cloned.1.call-start = ((), (), s32[]{:S(2)}) async-start(), calls=%async_computation.6 | async-start | bytes 4718592 | tf_op jit(solution)/shard_map/all_gather | solution.py:35
  10.0 103.0 %all-gather.6.cloned.1.call-start = ((), (), s32[]{:S(2)}) async-start(), calls=%async_computation.5 | async-start | bytes 4456448 | tf_op jit(solution)/shard_map/all_gather | solution.py:40
  45.4 2.8 copy-start.10
  45.4 2.7 copy-start.8
  45.4 72.6 %copy-start.6 = (f32[1,256]{1,0:T(1,128)}, f32[1,256]{1,0:T(1,128)S(1)}, u32[]{:S(2)}) copy-start(f32[1,256]{1,0:T(1,128)S(1)} %get-tuple-element.679) | copy-start | bytes 3076
  46.3 97.4 %all-gather.12.cloned.1.call-start = ((), (), s32[]{:S(2)}) async-start(), calls=%async_computation.8 | async-start | bytes 1572864 | tf_op jit(solution)/shard_map/all_gather | solution.py:36
  47.4 143.9 %all-gather.14.cloned.1.call-start = ((), (), s32[]{:S(2)}) async-start(), calls=%async_computation.9 | async-start | bytes 4456448 | tf_op jit(solution)/shard_map/all_gather | solution.py:116
  48.0 171.2 %reduce-scatter.5.cloned.1.call-start = ((), (), s32[]{:S(2)}) async-start(), calls=%async_computation.10 | async-start | bytes 786432 | tf_op jit(solution)/shard_map/reduce_scatter | solution.py:152
  143.7 62.6 %copy-start.2 = (bf16[512,128]{0,1:T(8,128)(2,1)}, bf16[512,128]{0,1:T(8,128)(2,1)S(1)}, u32[]{:S(2)}) copy-start(bf16[512,128]{0,1:T(8,128)(2,1)S(1)} %copy.49) | copy-start | bytes 393220
  206.3 36.1 %reduce-scatter.11.cloned.1.call-start = ((), (), s32[]{:S(2)}) async-start(), calls=%async_computation.13 | async-start | bytes 1572864 | tf_op jit(solution)/shard_map/reduce_scatter | solution.py:175
  210.3 79.1 %all-gather.10.cloned.1.call-start = ((), (), s32[]{:S(2)}) async-start(), calls=%async_computation.7 | async-start | bytes 2228224 | tf_op jit(solution)/shard_map/all_gather | solution.py:105
  211.0 153.8 %reduce-scatter.7.cloned.1.call-start = ((), (), s32[]{:S(2)}) async-start(), calls=%async_computation.11 | async-start | bytes 4456448 | tf_op jit(solution)/shard_map/reduce_scatter | solution.py:181
  226.1 6.4 %copy-start.1 = (bf16[128,4096]{0,1:T(8,128)(2,1)S(1)}, bf16[128,4096]{0,1:T(8,128)(2,1)}, u32[]{:S(2)}) copy-start(bf16[128,4096]{0,1:T(8,128)(2,1)} %all-gather.12.cloned.1.call-done) | copy-start | bytes 3145732
  226.1 184.1 %reduce-scatter.9.cloned.1.call-start = ((), (), s32[]{:S(2)}) async-start(), calls=%async_computation.12 | async-start | bytes 4718592 | tf_op jit(solution)/shard_map/reduce_scatter | solution.py:172
  233.8 36.5 %all-to-all-start = ((bf16[128,16,256]{2,0,1:T(8,128)(2,1)}), bf16[128,16,256]{2,0,1:T(8,128)(2,1)S(1)}, u32[]{:S(2)}, u32[]{:S(2)}) async-start(bf16[128,16,256]{2,0,1:T(8,128)(2,1)} %copy.51), calls=%async_computation | async-start | bytes 2097152 | tf_op jit(solution)/shard_map/all_to_all | solution.py:106
  289.4 75.4 %copy-start.7 = (f32[1,256]{1,0:T(1,128)S(1)}, f32[1,256]{1,0:T(1,128)}, u32[]{:S(2)}) copy-start(f32[1,256]{1,0:T(1,128)} %copy-done.6) | copy-start | bytes 3076
  289.4 75.4 %copy-start.9 = (f32[1,256]{1,0:T(1,128)S(1)}, f32[1,256]{1,0:T(1,128)}, u32[]{:S(2)}) copy-start(f32[1,256]{1,0:T(1,128)} %copy-done.8) | copy-start | bytes 3076
  289.4 75.4 %copy-start.11 = (pred[512]{0:T(512)(128)(4,1)S(1)}, pred[512]{0:T(512)(128)(4,1)}, u32[]{:S(2)}) copy-start(pred[512]{0:T(512)(128)(4,1)} %copy-done.10) | copy-start | bytes 1540
  294.2 102.4 %copy-start.13 = (s32[512]{0:T(512)S(1)}, s32[512]{0:T(512)}, u32[]{:S(2)}) copy-start(s32[512]{0:T(512)} %param.14) | copy-start | bytes 6148
  364.8 48.5 %copy-start.3 = (bf16[256,512]{0,1:T(8,128)(2,1)S(1)}, bf16[256,512]{0,1:T(8,128)(2,1)}, u32[]{:S(2)}) copy-start(bf16[256,512]{0,1:T(8,128)(2,1)} %reduce-scatter.7.cloned.1.call-done) | copy-start | bytes 786436
Sparse Core Ops, SparseCore 0:
  10.1 47.6 all-gather.7
  60.5 52.4 all-gather.5
  115.1 23.5 all-gather.11
  140.6 50.6 all-gather.13
  206.4 12.7 reduce-scatter.4
  221.9 20.3 reduce-scatter.10
  245.1 44.2 all-gather.9
  293.3 71.4 reduce-scatter.6
  367.6 42.5 reduce-scatter.8
where the time goes:
time: 421 us
  waiting for transfers between devices  243 us (58%)
  blocking collectives  85.3 us (20%)
  matrix products  40.2 us (10%)
  local copies, waits for them, and re-layouts  16.1 us (4%)
  between operations  14.2 us (3%)
  other arithmetic  11.5 us (3%)
  starting transfers between devices  6.02 us (1%)
  loops' own time  4.31 us (1%)
    reduce_scatter x1, waiting for transfers between devices, per_device(): lax.psum_scatter(jnp.einsum('mch,mth->ct', rows_block, grads, preferred_e...  67 us
    all_gather x1, waiting for transfers between devices, per_device(): lax.all_gather(normed, ('gx', 'gy'), axis=1, tiled=True)  55.2 us
    all_gather x1, waiting for transfers between devices, per_device(): segment = lax.all_gather(grad_out, ('gx', 'gy'), axis=1, tiled=True)  47.6 us
    psum x1, blocking collectives, per_device(): squares = lax.psum(jnp.sum(inputs_f * inputs_f, axis=1), ('gx', 'gy'))  35.2 us
    psum x1, blocking collectives, per_device(): norm_dots = lax.psum(jnp.sum(upstream * scaled, axis=1), ('gx', 'gy'))  30.5 us
    all_to_all x1, waiting for transfers between devices, per_device(): lax.all_to_all(wo_full, ('gx', 'gy'), split_axis=1, concat_axis=0, tiled=...  25.8 us
    all_gather x1, waiting for transfers between devices, per_device(): all_heads = lax.all_gather(attended, ('gx', 'gy'), axis=1, tiled=True)  19.1 us
    all_gather x1, blocking collectives, per_device(): lax.all_gather(jnp.concatenate([projected[1], projected[2]], axis=1), 'gz...  13.9 us
  transfers between devices with their start and end apart: 10, of which 9 were waited for; matrix products, arithmetic and copies ran while one was open for 11% of the time, Pallas kernels for 0%

commit v1 on v0

--- a/solution.py
+++ b/solution.py
@@ -6,6 +6,22 @@
 
 epsilon = 1e-05
 masked_low = -1e30
+
+
+def product_in_turn(shard, axis, dim, term):
+    size, here, extent = (lax.axis_size(axis), lax.axis_index(axis), shard.shape[dim])
+    upward = [(i, (i + 1) % size) for i in range(size)]
+    backward = [(i, (i - 1) % size) for i in range(size)]
+    half = size // 2
+    from_left = from_right = shard
+    subtotal = term(shard, here * extent)
+    for step in range(1, half + 1):
+        from_left = lax.ppermute(from_left, axis, upward)
+        if step < size - half:
+            from_right = lax.ppermute(from_right, axis, backward)
+            subtotal = subtotal + term(from_right, (here + step) % size * extent)
+        subtotal = subtotal + term(from_left, (here - step) % size * extent)
+    return subtotal
 
 
 def span_index(positions, image_spans):
@@ -35,11 +51,16 @@
     w_full = lax.all_gather(w_qkv, "gz", axis=1, tiled=True)
     wo_full = lax.all_gather(w_out, "gz", axis=1, tiled=True)
     rows_block = w_full
-    projected = jnp.einsum(
-        "tc,mch->mth",
-        lax.all_gather(normed, ("gx", "gy"), axis=1, tiled=True),
-        rows_block,
-        preferred_element_type=jnp.float32,
+    projected = product_in_turn(
+        normed,
+        ("gx", "gy"),
+        1,
+        lambda own_block, start: jnp.einsum(
+            "tc,mch->mth",
+            own_block,
+            lax.dynamic_slice_in_dim(rows_block, start, own_block.shape[1], axis=1),
+            preferred_element_type=jnp.float32,
+        ),
     )
     projected = projected.astype(jnp.bfloat16)
     queries = projected[0]

time: 421 us -> 468 us (1.11)
  waiting for transfers between devices: 243 us -> 192 us
  starting transfers between devices: 6.02 us -> 54.7 us
  blocking collectives: 85.3 us -> 131 us
    ppermute x0 -> x15, starting transfers between devices: none -> 54.1 us  [the longest x8 40.2 us: product_in_turn(): from_left = lax.ppermute(from_left, axis, upward)]
    all_gather x1, waiting for transfers between devices: 47.6 us -> 0.02 us  [per_device(): segment = lax.all_gather(grad_out, ('gx', 'gy'), axis=1, tiled=True)]
    ppermute x0 -> x15, waiting for transfers between devices: none -> 42.7 us  [the longest x8 26.9 us: product_in_turn(): from_left = lax.ppermute(from_left, axis, upward)]
    all_to_all x0 -> x1, blocking collectives: none -> 41.3 us  [per_device(): lax.all_to_all(wo_full, ('gx', 'gy'), split_axis=1, concat_axis=0, tiled=...]
    all_to_all x1 -> x0, waiting for transfers between devices: 25.8 us -> none  [per_device(): lax.all_to_all(wo_full, ('gx', 'gy'), split_axis=1, concat_axis=0, tiled=...]
    all_gather x1, waiting for transfers between devices: 19.1 us -> 0.01 us  [per_device(): all_heads = lax.all_gather(attended, ('gx', 'gy'), axis=1, tiled=True)]
    dot_general x0 -> x16, matrix products: none -> 9.97 us  [per_device(): jnp.einsum('tc,mch->mth', own_block, lax.dynamic_slice_in_dim(rows_block,...]
    reduce_scatter x1, waiting for transfers between devices: 3.11 us -> 12.9 us  [per_device(): lax.psum_scatter(partial_value.astype(jnp.bfloat16), 'gz', scatter_dimens...]
  transfers between devices with their start and end apart: 10 -> 24, of which waited for: 9 -> 18; matrix products, arithmetic and copies ran while one was open for 11% -> 11% of each run, Pallas kernels for 0% -> 0%
where the time goes in v1:
time: 468 us; the launch traced here: 467 us
  waiting for transfers between devices  192 us (41%)
  blocking collectives  131 us (28%)
  starting transfers between devices  54.7 us (12%)
  matrix products  42 us (9%)
  local copies, waits for them, and re-layouts  15.7 us (3%)
  between operations  14.7 us (3%)
  other arithmetic  12.5 us (3%)
    reduce_scatter x1, waiting for transfers between devices, per_device(): lax.psum_scatter(jnp.einsum('mch,mth->ct', rows_block, grads, preferred_e...  74.6 us
    all_gather x1, waiting for transfers between devices, per_device(): lax.all_gather(normed, ('gx', 'gy'), axis=1, tiled=True)  47.7 us
    all_to_all x1, blocking collectives, per_device(): lax.all_to_all(wo_full, ('gx', 'gy'), split_axis=1, concat_axis=0, tiled=...  41.3 us
    ppermute x8, starting transfers between devices, product_in_turn(): from_left = lax.ppermute(from_left, axis, upward)  40.2 us
    psum x1, blocking collectives, per_device(): squares = lax.psum(jnp.sum(inputs_f * inputs_f, axis=1), ('gx', 'gy'))  35.2 us
    psum x1, blocking collectives, per_device(): norm_dots = lax.psum(jnp.sum(upstream * scaled, axis=1), ('gx', 'gy'))  30.6 us
    ppermute x8, waiting for transfers between devices, product_in_turn(): from_left = lax.ppermute(from_left, axis, upward)  26.9 us
    all_gather x1, blocking collectives, per_device(): lax.all_gather(jnp.concatenate([projected[1], projected[2]], axis=1), 'gz...  18.2 us
  transfers between devices with their start and end apart: 24, of which 18 were waited for; matrix products, arithmetic and copies ran while one was open for 11% of the time, Pallas kernels for 0%

profile of v1, /device:TPU:0, one launch (start us, length us, event | category | flops | bytes accessed | tf_op | source)
XLA Modules:
  0.0 467.3 jit_solution(9484943557682374228)
XLA Ops:
  7.3 2.7 copy.44
  10.2 35.2 %psum.21 = f32[512]{0:T(512)S(1)} all-reduce(f32[512]{0:T(512)S(1)} %fusion.73), channel_id=1, replica_groups=mesh['gx'=4,'gy'=4,'gz'=2] {'gx','gy'}, use_global_device_ids=true, to_apply=%region_1.0 | all-reduce | flops 512 | bytes 4096 | tf_op jit(solution)/shard_map/psum | solution.py:46
  45.7 1.0 copy.50
  46.8 4.5 collective-permute-start
  51.3 5.3 %collective-permute-done.1 = bf16[512,256]{1,0:T(8,128)(2,1)S(1)} collective-permute-done((bf16[512,256]{1,0:T(8,128)(2,1)S(1)}, bf16[512,256]{1,0:T(8,128)(2,1)S(1)}, u32[]{:S(2)}, u32[]{:S(2)}) %collective-permute-start.1) | collective-permute-done | bytes 262176 | tf_op jit(solution)/shard_map/ppermute | solution.py:19
  56.5 2.6 collective-permute-done
  59.2 3.5 collective-permute-start.2
  62.6 3.5 collective-permute-done.3
  66.1 3.7 collective-permute-done.2
  69.9 4.0 collective-permute-start.4
  73.9 3.6 collective-permute-done.5
  77.5 2.7 collective-permute-start.7
  80.2 3.0 collective-permute-done.4
  83.3 5.7 %collective-permute-done.7 = bf16[512,256]{1,0:T(8,128)(2,1)S(1)} collective-permute-done((bf16[512,256]{1,0:T(8,128)(2,1)S(1)}, bf16[512,256]{1,0:T(8,128)(2,1)S(1)}, u32[]{:S(2)}, u32[]{:S(2)}) %collective-permute-start.7) | collective-permute-done | bytes 262176 | tf_op jit(solution)/shard_map/ppermute | solution.py:19
  89.0 5.2 %collective-permute-start.9 = (bf16[512,256]{1,0:T(8,128)(2,1)S(1)}, bf16[512,256]{1,0:T(8,128)(2,1)S(1)}, u32[]{:S(2)}, u32[]{:S(2)}) collective-permute-start(bf16[512,256]{1,0:T(8,128)(2,1)S(1)} %collective-permute-done.7), channel_id=1, source_target_pairs={{0,2},{2,4},{4,6},{6,8},{8,10},{10,12},{12,14},{14,16},{16,18},{18... | collective-permute-start | bytes 786440 | tf_op jit(solution)/shard_map/ppermute | solution.py:19
  94.3 1.4 collective-permute-done.6
  95.7 1.3 collective-permute-start.8
  97.1 1.5 collective-permute-done.9
  98.6 11.9 %collective-permute-start.11 = (bf16[512,256]{1,0:T(8,128)(2,1)S(1)}, bf16[512,256]{1,0:T(8,128)(2,1)}, u32[]{:S(2)}, u32[]{:S(2)}) collective-permute-start(bf16[512,256]{1,0:T(8,128)(2,1)S(1)} %collective-permute-done.9), channel_id=1, source_target_pairs={{0,2},{2,4},{4,6},{6,8},{8,10},{10,12},{12,14},{14,16},{16,18},{18... | collective-permute-start | bytes 786440 | tf_op jit(solution)/shard_map/ppermute | solution.py:19
  110.5 3.3 collective-permute-done.8
  113.8 4.7 %collective-permute-done.11 = bf16[512,256]{1,0:T(8,128)(2,1)} collective-permute-done((bf16[512,256]{1,0:T(8,128)(2,1)S(1)}, bf16[512,256]{1,0:T(8,128)(2,1)}, u32[]{:S(2)}, u32[]{:S(2)}) %collective-permute-start.11) | collective-permute-done | bytes 262176 | tf_op jit(solution)/shard_map/ppermute | solution.py:19
  118.5 8.4 %collective-permute-start.13 = (bf16[512,256]{1,0:T(8,128)(2,1)}, bf16[512,256]{1,0:T(8,128)(2,1)}, u32[]{:S(2)}, u32[]{:S(2)}) collective-permute-start(bf16[512,256]{1,0:T(8,128)(2,1)} %collective-permute-done.11), channel_id=1, source_target_pairs={{0,2},{2,4},{4,6},{6,8},{8,10},{10,12},{12,14},{14,16},{16,18},{18... | collective-permute-start | bytes 786440 | tf_op jit(solution)/shard_map/ppermute | solution.py:19
  127.3 1.7 collective-permute-done.10
  129.6 2.6 collective-permute-done.13
  132.2 11.9 %collective-permute-start.14 = (bf16[512,256]{1,0:T(8,128)(2,1)}, bf16[512,256]{1,0:T(8,128)(2,1)}, u32[]{:S(2)}, u32[]{:S(2)}) collective-permute-start(bf16[512,256]{1,0:T(8,128)(2,1)} %collective-permute-done.13), channel_id=1, source_target_pairs={{0,2},{2,4},{4,6},{6,8},{8,10},{10,12},{12,14},{14,16},{16,18},{18... | collective-permute-start | bytes 786440 | tf_op jit(solution)/shard_map/ppermute | solution.py:19
  144.2 1.5 fusion.81
  145.7 1.4 fusion.84
  147.0 1.4 fusion.87
  151.4 1.2 fusion.78
  153.0 1.3 fusion.62
  154.3 18.2 %all_gather.19 = bf16[1024,256]{0,1:T(8,128)(2,1)S(1)} all-gather(bf16[512,256]{0,1:T(8,128)(2,1)S(1)} %pad_maximum_fusion.1), channel_id=1, replica_groups=mesh['gx'=4,'gy'=4,'gz'=2] {'gz'}, dimensions={0}, use_global_device_ids=true | all-gather | bytes 786432 | tf_op jit(solution)/shard_map/all_gather | solution.py:67
  172.9 4.8 %while.43 = (s32[]{:T(128)}, f32[512]{0:T(512)S(1)}, f32[512]{0:T(512)S(1)}, s32[2]{0:T(128)S(1)}, s32[512]{0:T(512)S(1)}, /*index=5*/s32[2,8]{1,0:T(2,128)S(1)}...) while((s32[]{:T(128)}, f32[512]{0:T(512)S(1)}, ...), condition=%wide.region_7.8_spmd.clone, body=%wide.region_3.7_spmd.clone.sunk | while | flops 70803472 | bytes 2418646 | solution.py:105
  172.9 0.6 dynamic_slice.142
  175.3 0.6 dynamic_slice.142
  177.7 4.5 while.44
  177.8 0.6 dynamic_slice.143
  179.1 0.9 fusion.178
  180.0 0.6 dynamic_slice.143
  181.4 0.9 fusion.178
  182.4 4.0 multiply_reduce_fusion
  186.6 8.0 %while.45 = (s32[]{:T(128)}, f32[512,128]{1,0:T(8,128)S(1)}, bf16[2,512,256]{1,2,0:T(8,128)(2,1)}, s32[2]{0:T(128)S(1)}, s32[512]{0:T(512)S(1)}, /*index=5*/s32[...) while((s32[]{:T(128)}, f32[512,128]{1,0:T(8,128)S(1)}, ...), condition=%wide.region_15.16_spmd.clone, body=%wide.region_13.15_spmd.clone.sunk | while | flops 339367424 | bytes 6974993 | solution.py:170
  189.9 0.7 fusion.193
  193.9 0.7 fusion.193
  194.6 2.0 copy.56
  197.9 3.9 convolution_convert_fusion.1
  201.8 9.2 %reduce-scatter.5.cloned.1.call-done = bf16[512,256]{1,0:T(8,128)(2,1)} async-done(((bf16[1024,256]{1,0:T(8,128)(2,1)}), bf16[512,256]{1,0:T(8,128)(2,1)}) %reduce-scatter.5.cloned.1.call-update) | async-done | bytes 262160 | tf_op jit(solution)/shard_map/reduce_scatter | solution.py:173
  211.0 1.0 slice_bitcast_fusion.7
  212.0 5.7 %fusion.52 = bf16[4096,512]{0,1:T(8,128)(2,1)} fusion(bf16[3,4096,128]{1,2,0:T(8,128)(2,1)} %all-gather.6.cloned.1.call-done, bf16[1,512,128]{2,1,0:T(8,128)(2,1)S(1)} %get-tuple-element.678, bf16[1,512,128]{2,1,0:T(8,128)(2,1)S(1)} %get-tuple-element.677, bf16[1,512,128]{2,1,0:T(8,128)(2,1)S(1)} %convert_bitcast_fusion), kind=kOutput, calls=%fused_computation.84 | convolution fusion | flops 1613103104 | bytes 7733248 | tf_op jit(solution)/shard_map/mch,mth->ct/dot_general | solution.py:203
  217.8 47.7 %all-gather.14.cloned.1.call-done = bf16[512,4096]{1,0:T(8,128)(2,1)} async-done(((bf16[512,256]{1,0:T(8,128)(2,1)}), bf16[512,4096]{1,0:T(8,128)(2,1)}) %all-gather.14.cloned.1.call-update) | async-done | bytes 4194320 | tf_op jit(solution)/shard_map/all_gather | solution.py:188
  265.4 5.7 %fusion.53 = bf16[3,4096,128]{1,2,0:T(8,128)(2,1)} fusion(bf16[512,4096]{1,0:T(8,128)(2,1)} %all-gather.14.cloned.1.call-done, bf16[1,512,128]{2,1,0:T(8,128)(2,1)S(1)} %get-tuple-element.678, bf16[1,512,128]{2,1,0:T(8,128)(2,1)S(1)} %get-tuple-element.677, bf16[1,512,128]{2,1,0:T(8,128)(2,1)S(1)} %convert_bitcast_fusion), kind=kOutput, calls=%fused_computation.85 | convolution fusion | flops 1612578816 | bytes 7733248 | tf_op jit(solution)/shard_map/tc,mth->mch/dot_general | solution.py:186
  271.2 1.2 copy-done.1
  272.9 41.3 %all_to_all.16 = bf16[128,16,256]{2,0,1:T(8,128)(2,1)S(1)} all-to-all(bf16[128,16,256]{2,0,1:T(8,128)(2,1)S(1)} %copy.51), channel_id=1, replica_groups=mesh['gx'=4,'gy'=4,'gz'=2] {'gx','gy'}, dimensions={1} | all-to-all | bytes 2097152 | tf_op jit(solution)/shard_map/all_to_all | solution.py:127
  314.2 4.9 %convolution_convert_fusion.2 = bf16[16,512,256]{2,1,0:T(8,128)(2,1)} fusion(bf16[512,16,128]{0,2,1:T(8,128)(2,1)} %bitcast.189, bf16[128,16,256]{2,0,1:T(8,128)(2,1)S(1)} %all_to_all.16), kind=kOutput, calls=%fused_computation.88 | convolution fusion | flops 538968064 | bytes 7340032 | tf_op jit(solution)/shard_map/thd,hdc->htc/dot_general | solution.py:129
  319.1 3.7 reduce_sum.98
  322.8 12.9 %reduce-scatter.11.cloned.1.call-done = bf16[128,2048]{1,0:T(8,128)(2,1)} async-done(((bf16[128,4096]{1,0:T(8,128)(2,1)}), bf16[128,2048]{1,0:T(8,128)(2,1)}) %reduce-scatter.11.cloned.1.call-update) | async-done | bytes 524304 | tf_op jit(solution)/shard_map/reduce_scatter | solution.py:196
  335.6 2.1 convert_element_type.100
  337.7 74.6 %reduce-scatter.7.cloned.1.call-done = bf16[256,512]{0,1:T(8,128)(2,1)} async-done(((bf16[4096,512]{0,1:T(8,128)(2,1)}), bf16[256,512]{0,1:T(8,128)(2,1)}) %reduce-scatter.7.cloned.1.call-update) | async-done | bytes 262160 | tf_op jit(solution)/shard_map/reduce_scatter | solution.py:202
  412.3 1.2 fusion.67
  413.6 30.6 %psum.22 = f32[512]{0:T(512)S(1)} all-reduce(f32[512]{0:T(512)S(1)} %fusion.67), channel_id=1, replica_groups=mesh['gx'=4,'gy'=4,'gz'=2] {'gx','gy'}, use_global_device_ids=true, to_apply=%region_19.20 | all-reduce | flops 512 | bytes 4096 | tf_op jit(solution)/shard_map/psum | solution.py:214
  444.1 1.5 fusion.71
  445.6 5.7 %psum.23 = f32[2,256]{1,0:T(2,128)} all-reduce(f32[2,256]{1,0:T(2,128)S(1)} %fusion.71), channel_id=1, replica_groups=mesh['gx'=4,'gy'=4,'gz'=2] {'gz'}, use_global_device_ids=true, to_apply=%region_22.23 | all-reduce | flops 512 | bytes 4096 | tf_op jit(solution)/shard_map/psum | solution.py:220
  451.3 1.9 fusion.70
  453.2 4.4 reduce-scatter.9.cloned.1.call-done
  457.7 3.1 copy.59
  (164 shorter events, 14.8 us)
Async XLA Ops:
  7.2 2.8 copy-start
  7.2 38.2 %copy-start.16 = (s32[512]{0:T(512)S(1)}, s32[512]{0:T(512)}, u32[]{:S(2)}) copy-start(s32[512]{0:T(512)} %param.14) | copy-start | bytes 6148
  7.2 38.2 %copy-start.18 = (f32[2,256]{1,0:T(2,128)S(1)}, f32[2,256]{1,0:T(2,128)}, u32[]{:S(2)}) copy-start(f32[2,256]{1,0:T(2,128)} %param.16) | copy-start | bytes 6148
  7.2 38.5 %copy-start.6 = (bf16[128,2048]{1,0:T(8,128)(2,1)S(1)}, bf16[128,2048]{1,0:T(8,128)(2,1)}, u32[]{:S(2)}) copy-start(bf16[128,2048]{1,0:T(8,128)(2,1)} %param.18) | copy-start | bytes 1572868
  7.2 103.3 %copy-start.7 = (s32[2,8]{1,0:T(2,128)S(1)}, s32[2,8]{1,0:T(2,128)}, u32[]{:S(2)}) copy-start(s32[2,8]{1,0:T(2,128)} %param.15) | copy-start | bytes 196
  7.2 136.9 %all-gather.6.cloned.1.call-start = ((), (), s32[]{:S(2)}) async-start(), calls=%async_computation.5 | async-start | bytes 4718592 | tf_op jit(solution)/shard_map/all_gather | solution.py:51
  10.0 172.4 %all-gather.10.cloned.1.call-start = ((), (), s32[]{:S(2)}) async-start(), calls=%async_computation.7 | async-start | bytes 1572864 | tf_op jit(solution)/shard_map/all_gather | solution.py:52
  45.4 5.9 %copy-start.14 = (pred[512]{0:T(512)(128)(4,1)}, pred[512]{0:T(512)(128)(4,1)S(1)}, u32[]{:S(2)}) copy-start(pred[512]{0:T(512)(128)(4,1)S(1)} %broadcast_compare_fusion.3) | copy-start | bytes 1540
  45.4 81.9 %copy-start.12 = (f32[1,256]{1,0:T(1,128)}, f32[1,256]{1,0:T(1,128)S(1)}, u32[]{:S(2)}) copy-start(f32[1,256]{1,0:T(1,128)S(1)} %get-tuple-element.680) | copy-start | bytes 3076
  45.6 103.4 %copy-start.5 = (bf16[512,256]{1,0:T(8,128)(2,1)}, bf16[512,256]{1,0:T(8,128)(2,1)S(1)}, u32[]{:S(2)}) copy-start(bf16[512,256]{1,0:T(8,128)(2,1)S(1)} %fusion.74) | copy-start | bytes 786436
  45.6 10.9 %collective-permute-start.1 = (bf16[512,256]{1,0:T(8,128)(2,1)S(1)}, bf16[512,256]{1,0:T(8,128)(2,1)S(1)}, u32[]{:S(2)}, u32[]{:S(2)}) collective-permute-start(bf16[512,256]{1,0:T(8,128)(2,1)S(1)} %fusion.74), channel_id=1, source_target_pairs={{0,2},{2,4},{4,6},{6,8},{8,10},{10,12},{12,14},{14,16},{16,18},{18... | collective-permute-start | bytes 786440 | tf_op jit(solution)/shard_map/ppermute | solution.py:19
  46.7 135.7 %all-gather.12.cloned.1.call-start = ((), (), s32[]{:S(2)}) async-start(), calls=%async_computation.8 | async-start | bytes 4456448 | tf_op jit(solution)/shard_map/all_gather | solution.py:137
  46.8 12.4 %collective-permute-start = (bf16[512,256]{1,0:T(8,128)(2,1)S(1)}, bf16[512,256]{1,0:T(8,128)(2,1)S(1)}, u32[]{:S(2)}, u32[]{:S(2)}) collective-permute-start(bf16[512,256]{1,0:T(8,128)(2,1)S(1)} %fusion.74), channel_id=1, source_target_pairs={{0,30},{2,0},{4,2},{6,4},{8,6},{10,8},{12,10},{14,12},{16,14},{18,... | collective-permute-start | bytes 786440 | tf_op jit(solution)/shard_map/ppermute | solution.py:21
  56.5 9.6 %collective-permute-start.3 = (bf16[512,256]{1,0:T(8,128)(2,1)S(1)}, bf16[512,256]{1,0:T(8,128)(2,1)S(1)}, u32[]{:S(2)}, u32[]{:S(2)}) collective-permute-start(bf16[512,256]{1,0:T(8,128)(2,1)S(1)} %collective-permute-done.1), channel_id=1, source_target_pairs={{0,2},{2,4},{4,6},{6,8},{8,10},{10,12},{12,14},{14,16},{16,18},{18... | collective-permute-start | bytes 786440 | tf_op jit(solution)/shard_map/ppermute | solution.py:19
  59.2 10.7 %collective-permute-start.2 = (bf16[512,256]{1,0:T(8,128)(2,1)S(1)}, bf16[512,256]{1,0:T(8,128)(2,1)S(1)}, u32[]{:S(2)}, u32[]{:S(2)}) collective-permute-start(bf16[512,256]{1,0:T(8,128)(2,1)S(1)} %collective-permute-done), channel_id=1, source_target_pairs={{0,30},{2,0},{4,2},{6,4},{8,6},{10,8},{12,10},{14,12},{16,14},{18,... | collective-permute-start | bytes 786440 | tf_op jit(solution)/shard_map/ppermute | solution.py:21
  66.1 11.3 %collective-permute-start.5 = (bf16[512,256]{1,0:T(8,128)(2,1)S(1)}, bf16[512,256]{1,0:T(8,128)(2,1)S(1)}, u32[]{:S(2)}, u32[]{:S(2)}) collective-permute-start(bf16[512,256]{1,0:T(8,128)(2,1)S(1)} %collective-permute-done.3), channel_id=1, source_target_pairs={{0,2},{2,4},{4,6},{6,8},{8,10},{10,12},{12,14},{14,16},{16,18},{18... | collective-permute-start | bytes 786440 | tf_op jit(solution)/shard_map/ppermute | solution.py:19
  69.9 13.3 %collective-permute-start.4 = (bf16[512,256]{1,0:T(8,128)(2,1)S(1)}, bf16[512,256]{1,0:T(8,128)(2,1)S(1)}, u32[]{:S(2)}, u32[]{:S(2)}) collective-permute-start(bf16[512,256]{1,0:T(8,128)(2,1)S(1)} %collective-permute-done.2), channel_id=1, source_target_pairs={{0,30},{2,0},{4,2},{6,4},{8,6},{10,8},{12,10},{14,12},{16,14},{18,... | collective-permute-start | bytes 786440 | tf_op jit(solution)/shard_map/ppermute | solution.py:21
  77.5 16.8 %copy-start.8 = (bf16[512,256]{1,0:T(8,128)(2,1)}, bf16[512,256]{1,0:T(8,128)(2,1)S(1)}, u32[]{:S(2)}) copy-start(bf16[512,256]{1,0:T(8,128)(2,1)S(1)} %collective-permute-done.5) | copy-start | bytes 786436
  77.5 11.5 %collective-permute-start.7 = (bf16[512,256]{1,0:T(8,128)(2,1)S(1)}, bf16[512,256]{1,0:T(8,128)(2,1)S(1)}, u32[]{:S(2)}, u32[]{:S(2)}) collective-permute-start(bf16[512,256]{1,0:T(8,128)(2,1)S(1)} %collective-permute-done.5), channel_id=1, source_target_pairs={{0,2},{2,4},{4,6},{6,8},{8,10},{10,12},{12,14},{14,16},{16,18},{18... | collective-permute-start | bytes 786440 | tf_op jit(solution)/shard_map/ppermute | solution.py:19
  83.2 12.6 %collective-permute-start.6 = (bf16[512,256]{1,0:T(8,128)(2,1)S(1)}, bf16[512,256]{1,0:T(8,128)(2,1)S(1)}, u32[]{:S(2)}, u32[]{:S(2)}) collective-permute-start(bf16[512,256]{1,0:T(8,128)(2,1)S(1)} %collective-permute-done.4), channel_id=1, source_target_pairs={{0,30},{2,0},{4,2},{6,4},{8,6},{10,8},{12,10},{14,12},{16,14},{18,... | collective-permute-start | bytes 786440 | tf_op jit(solution)/shard_map/ppermute | solution.py:21
  89.0 38.2 %copy-start.10 = (bf16[512,256]{1,0:T(8,128)(2,1)}, bf16[512,256]{1,0:T(8,128)(2,1)S(1)}, u32[]{:S(2)}) copy-start(bf16[512,256]{1,0:T(8,128)(2,1)S(1)} %collective-permute-done.7) | copy-start | bytes 786436
  89.0 9.6 %collective-permute-start.9 = (bf16[512,256]{1,0:T(8,128)(2,1)S(1)}, bf16[512,256]{1,0:T(8,128)(2,1)S(1)}, u32[]{:S(2)}, u32[]{:S(2)}) collective-permute-start(bf16[512,256]{1,0:T(8,128)(2,1)S(1)} %collective-permute-done.7), channel_id=1, source_target_pairs={{0,2},{2,4},{4,6},{6,8},{8,10},{10,12},{12,14},{14,16},{16,18},{18... | collective-permute-start | bytes 786440 | tf_op jit(solution)/shard_map/ppermute | solution.py:19
  94.2 116.7 %reduce-scatter.5.cloned.1.call-start = ((), (), s32[]{:S(2)}) async-start(), calls=%async_computation.9 | async-start | bytes 786432 | tf_op jit(solution)/shard_map/reduce_scatter | solution.py:173
  95.7 18.1 %collective-permute-start.8 = (bf16[512,256]{1,0:T(8,128)(2,1)S(1)}, bf16[512,256]{1,0:T(8,128)(2,1)S(1)}, u32[]{:S(2)}, u32[]{:S(2)}) collective-permute-start(bf16[512,256]{1,0:T(8,128)(2,1)S(1)} %collective-permute-done.6), channel_id=1, source_target_pairs={{0,30},{2,0},{4,2},{6,4},{8,6},{10,8},{12,10},{14,12},{16,14},{18,... | collective-permute-start | bytes 786440 | tf_op jit(solution)/shard_map/ppermute | solution.py:21
  98.6 28.7 %copy-start.11 = (bf16[512,256]{1,0:T(8,128)(2,1)}, bf16[512,256]{1,0:T(8,128)(2,1)S(1)}, u32[]{:S(2)}) copy-start(bf16[512,256]{1,0:T(8,128)(2,1)S(1)} %collective-permute-done.9) | copy-start | bytes 786436
  98.6 19.9 %collective-permute-start.11 = (bf16[512,256]{1,0:T(8,128)(2,1)S(1)}, bf16[512,256]{1,0:T(8,128)(2,1)}, u32[]{:S(2)}, u32[]{:S(2)}) collective-permute-start(bf16[512,256]{1,0:T(8,128)(2,1)S(1)} %collective-permute-done.9), channel_id=1, source_target_pairs={{0,2},{2,4},{4,6},{6,8},{8,10},{10,12},{12,14},{14,16},{16,18},{18... | collective-permute-start | bytes 786440 | tf_op jit(solution)/shard_map/ppermute | solution.py:19
  113.8 15.2 %collective-permute-start.10 = (bf16[512,256]{1,0:T(8,128)(2,1)S(1)}, bf16[512,256]{1,0:T(8,128)(2,1)S(1)}, u32[]{:S(2)}, u32[]{:S(2)}) collective-permute-start(bf16[512,256]{1,0:T(8,128)(2,1)S(1)} %collective-permute-done.8), channel_id=1, source_target_pairs={{0,30},{2,0},{4,2},{6,4},{8,6},{10,8},{12,10},{14,12},{16,14},{18,... | collective-permute-start | bytes 786440 | tf_op jit(solution)/shard_map/ppermute | solution.py:21
  118.5 13.7 %collective-permute-start.13 = (bf16[512,256]{1,0:T(8,128)(2,1)}, bf16[512,256]{1,0:T(8,128)(2,1)}, u32[]{:S(2)}, u32[]{:S(2)}) collective-permute-start(bf16[512,256]{1,0:T(8,128)(2,1)} %collective-permute-done.11), channel_id=1, source_target_pairs={{0,2},{2,4},{4,6},{6,8},{8,10},{10,12},{12,14},{14,16},{16,18},{18... | collective-permute-start | bytes 786440 | tf_op jit(solution)/shard_map/ppermute | solution.py:19
  129.0 23.7 %collective-permute-start.12 = (bf16[512,256]{1,0:T(8,128)(2,1)S(1)}, bf16[512,256]{1,0:T(8,128)(2,1)S(1)}, u32[]{:S(2)}, u32[]{:S(2)}) collective-permute-start(bf16[512,256]{1,0:T(8,128)(2,1)S(1)} %collective-permute-done.10), channel_id=1, source_target_pairs={{0,30},{2,0},{4,2},{6,4},{8,6},{10,8},{12,10},{14,12},{16,14},{18,... | collective-permute-start | bytes 786440 | tf_op jit(solution)/shard_map/ppermute | solution.py:21
  132.2 20.8 %collective-permute-start.14 = (bf16[512,256]{1,0:T(8,128)(2,1)}, bf16[512,256]{1,0:T(8,128)(2,1)}, u32[]{:S(2)}, u32[]{:S(2)}) collective-permute-start(bf16[512,256]{1,0:T(8,128)(2,1)} %collective-permute-done.13), channel_id=1, source_target_pairs={{0,2},{2,4},{4,6},{6,8},{8,10},{10,12},{12,14},{14,16},{16,18},{18... | collective-permute-start | bytes 786440 | tf_op jit(solution)/shard_map/ppermute | solution.py:19
  144.2 4.2 copy-start.2
  144.2 4.2 copy-start.9
  182.4 4.1 copy-start.3
  186.6 11.3 %copy-start.4 = (bf16[512,128]{0,1:T(8,128)(2,1)S(1)}, bf16[512,128]{0,1:T(8,128)(2,1)}, u32[]{:S(2)}) copy-start(bf16[512,128]{0,1:T(8,128)(2,1)} %copy-done.3) | copy-start | bytes 393220
  196.6 68.8 %all-gather.14.cloned.1.call-start = ((), (), s32[]{:S(2)}) async-start(), calls=%async_computation.11 | async-start | bytes 4456448 | tf_op jit(solution)/shard_map/all_gather | solution.py:188
  197.2 117.0 %all-gather.8.cloned.1.call-start = ((), (), s32[]{:S(2)}) async-start(), calls=%async_computation.6 | async-start | bytes 2228224 | tf_op jit(solution)/shard_map/all_gather | solution.py:126
  197.8 137.8 %reduce-scatter.11.cloned.1.call-start = ((), (), s32[]{:S(2)}) async-start(), calls=%async_computation.13 | async-start | bytes 1572864 | tf_op jit(solution)/shard_map/reduce_scatter | solution.py:196
  201.8 210.5 %reduce-scatter.7.cloned.1.call-start = ((), (), s32[]{:S(2)}) async-start(), calls=%async_computation.10 | async-start | bytes 4456448 | tf_op jit(solution)/shard_map/reduce_scatter | solution.py:202
  217.7 239.9 %reduce-scatter.9.cloned.1.call-start = ((), (), s32[]{:S(2)}) async-start(), calls=%async_computation.12 | async-start | bytes 4718592 | tf_op jit(solution)/shard_map/reduce_scatter | solution.py:193
  271.1 1.2 copy-start.1
  319.1 93.2 %copy-start.13 = (f32[1,256]{1,0:T(1,128)S(1)}, f32[1,256]{1,0:T(1,128)}, u32[]{:S(2)}) copy-start(f32[1,256]{1,0:T(1,128)} %copy-done.12) | copy-start | bytes 3076
  319.1 93.2 %copy-start.15 = (pred[512]{0:T(512)(128)(4,1)S(1)}, pred[512]{0:T(512)(128)(4,1)}, u32[]{:S(2)}) copy-start(pred[512]{0:T(512)(128)(4,1)} %copy-done.14) | copy-start | bytes 1540
  319.1 125.0 %copy-start.17 = (s32[512]{0:T(512)S(1)}, s32[512]{0:T(512)}, u32[]{:S(2)}) copy-start(s32[512]{0:T(512)} %param.14) | copy-start | bytes 6148
Sparse Core Ops, SparseCore 0:
  10.1 47.6 all-gather.5
  59.9 21.2 all-gather.9
  94.4 75.1 all-gather.11
  196.8 14.1 reduce-scatter.4
  212.9 52.4 all-gather.13
  268.1 45.3 all-gather.7
  316.3 19.3 reduce-scatter.10
  339.5 72.7 reduce-scatter.6
  415.1 42.4 reduce-scatter.8
